TPU v7x, 32 devices: a whole 2x2x4 slice. The times are simulated.
32 devices in a mesh: dp: 4 (over y, x), expert: 8 (over z, core).
Axes of the slice: x: 2, y: 2, z: 4, core: 2. Of those that a mesh axis runs over, the one named last changes fastest.
Arguments:
- shortcut_in: bfloat16 [128, 7168], P('expert', 'dp'), may hold values from -6 to 6
- current_in: bfloat16 [128, 7168], P('expert', 'dp'), may hold values from -6 to 6
- expert_ids: int32 [128, 4], P('expert'), may hold values from 0 to 7, all different within a row; in each aligned block of 16 rows (0 to 15, 16 to 31, ...) at most 12 rows name the same one
- route_weight: float32 [128, 4], P('expert'), may hold values from 0.1 to 1
- gate_weight: bfloat16 [8, 7168, 2048], P('expert', 'dp'), may hold values from -0.09375 to 0.09375
- up_weight: bfloat16 [8, 7168, 2048], P('expert', 'dp'), may hold values from -0.09375 to 0.09375
- down_weight: bfloat16 [8, 2048, 7168], P('expert', None, 'dp'), may hold values from -0.125 to 0.125
- shared_gate: bfloat16 [7168, 2048], P('dp'), may hold values from -0.09375 to 0.09375
- shared_up: bfloat16 [7168, 2048], P('dp'), may hold values from -0.09375 to 0.09375
- shared_down: bfloat16 [2048, 7168], P(None, 'dp'), may hold values from -0.125 to 0.125
Outputs:
- mixed: bfloat16 [128, 7168], P('expert', 'dp')
Inputs may be any that keep to these rules, and one draw needn't show every extreme that they name: `expert_ids`: each row names 4 different experts. In each aligned block of 16 rows (the tokens of one index of the expert axis) no expert is named by more than 12 rows, and in at least one such block some expert is named by exactly 12 rows.
All inputs are finite; a program needn't handle non-finite values.
Results may differ from a plain program's by a relative error of at most 0.035.
Values may be sent and summed in bfloat16 or wider, within the bound.
A program may use at most 128 MiB of HBM per device.

v0:
```python
import functools

import jax
import jax.numpy as jnp
from jax import lax
from jax.experimental import pallas as pl
from jax.experimental.pallas import tpu as pltpu
from jax.sharding import PartitionSpec as P


def activate(summed):
    return (jax.nn.silu(summed[:, 0]) * summed[:, 1]).astype(jnp.bfloat16)


def hidden_of(partial_value):
    summed = lax.psum_scatter(
        partial_value.astype(jnp.bfloat16), "dp", scatter_dimension=2, tiled=True
    ).astype(jnp.float32)
    return lax.all_gather(activate(summed), "dp", axis=1, tiled=True)


def send_rows(outgoing):
    return lax.all_to_all(outgoing, "expert", split_axis=0, concat_axis=0, tiled=True)


def expert_partial(arrived, gate_weight, up_weight):
    gate = jnp.einsum("sacd,adh->sach", arrived, gate_weight, preferred_element_type=jnp.float32)
    upper = jnp.einsum("sacd,adh->sach", arrived, up_weight, preferred_element_type=jnp.float32)
    stacked = jnp.stack([gate, upper], axis=3)
    return stacked.reshape(-1, 2, gate_weight.shape[2])


def local(
    shortcut_in,
    current_in,
    expert_ids,
    route_weight,
    gate_weight,
    up_weight,
    down_weight,
    shared_gate,
    shared_up,
    shared_down,
):
    sources = lax.axis_size("expert")
    local_experts = gate_weight.shape[0]
    experts = sources * local_experts
    tokens, top = expert_ids.shape
    capacity = 3 * tokens * top // (2 * experts)
    width = shortcut_in.shape[1]
    hidden_units = gate_weight.shape[2]
    flat_ids = expert_ids.reshape(-1)
    onehot = (flat_ids[:, None] == jnp.arange(experts, dtype=jnp.int32)[None, :]).astype(jnp.int32)
    rank = jnp.sum((jnp.cumsum(onehot, axis=0) - 1) * onehot, axis=1)
    slot = (flat_ids * capacity + rank).reshape(tokens, top)
    positions = jnp.arange(experts * capacity, dtype=jnp.int32)
    place = jnp.sum((slot[None, :, :] == positions[:, None, None]).astype(jnp.bfloat16), axis=2)
    outgoing = jnp.dot(place, shortcut_in, preferred_element_type=jnp.float32).astype(jnp.bfloat16)
    outgoing = outgoing.reshape(sources, local_experts * capacity, width)
    shared_gate_sum = jnp.dot(current_in, shared_gate, preferred_element_type=jnp.float32)
    shared_up_sum = jnp.dot(current_in, shared_up, preferred_element_type=jnp.float32)
    shared_partial = jnp.stack([shared_gate_sum, shared_up_sum], axis=1)
    routed_rows = experts * capacity
    arrived = send_rows(outgoing).reshape(sources, local_experts, capacity, width)
    routed_partial = expert_partial(arrived, gate_weight, up_weight)
    joined = hidden_of(jnp.concatenate([routed_partial, shared_partial], axis=0))
    routed_hidden = joined[:routed_rows]
    shared_hidden = joined[routed_rows:]
    routed_hidden = routed_hidden.reshape(sources, local_experts, capacity, hidden_units)
    expert_out = jnp.einsum(
        "sach,ahd->sacd", routed_hidden, down_weight, preferred_element_type=jnp.float32
    ).astype(jnp.bfloat16)
    returned = lax.all_to_all(
        expert_out.reshape(sources, local_experts * capacity, width),
        "expert",
        split_axis=0,
        concat_axis=0,
        tiled=True,
    )
    picked = returned.reshape(routed_rows, width)[slot]
    routed = jnp.sum(route_weight[:, :, None] * picked.astype(jnp.float32), axis=1)
    shared_out = jnp.dot(shared_hidden, shared_down, preferred_element_type=jnp.float32)
    return (shared_out + routed).astype(jnp.bfloat16)


MESH = pl.DeviceIdType.MESH
BF = jnp.bfloat16
F32 = jnp.float32
PARTS = 2


def dot(a, b):
    return jnp.dot(a, b, preferred_element_type=F32)


def layer_kernel(
    n_dp, n_e, rows,
    x_ref, cur_ref, ids_ref, w_ref, gate_hbm, up_hbm, down_hbm, sg_hbm, su_hbm, sd_hbm,
    out_ref,
    gate_v, up_v, down_v, sg_v, su_v, sd_v,
    flip, m_own, m_all, x_all, c_all, xc, part, rs_in, hid, acc, shv,
    sh_part, sh_in, sh_hid, own_sum, contrib, pair_in, fin_out, fin_in,
    gate_sem, up_sem, down_sem, shw_sem,
    m_s, m_r, x_s, x_r, c_s, c_r, mp_s, mp_r, xp_s, xp_r, cp_s, cp_r,
    rs_s, rs_r, hid_s, hid_r, shp_s, shp_r, shh_s, shh_r, pair_s, pair_r, fin_s, fin_r,
):
    me_d = lax.axis_index("dp")
    me_e = lax.axis_index("expert")
    zs = n_e // 2
    z, c = me_e // 2, lax.rem(me_e, 2)
    pairs = zs // 2
    p, b = z // 2, lax.rem(z, 2)
    partner = 2 * z + (1 - c)
    tokens, width = x_ref.shape
    chunk = gate_v.shape[2]
    hs = chunk * PARTS
    total = n_e * tokens
    sh = sg_v.shape[1]
    share = total // n_dp
    slots = [(q, s) for q in range(PARTS) for s in [*range(1, n_dp), 0]]

    def start(copy):
        copy.start()
        return copy

    def dp_dev(s):
        return lax.rem(me_d + s, n_dp)

    def dp_src(s):
        return lax.rem(me_d - s + n_dp, n_dp)

    def z_dev(s):
        return 2 * (2 * lax.rem(p + s // 2, pairs) + lax.rem(b + s % 2, 2)) + c

    def z_src(s):
        return 2 * (2 * lax.rem(p - s // 2 + pairs, pairs) + lax.rem(b + s % 2, 2)) + c

    def group_blocks(a):
        return pl.ds(4 * lax.rem(p - a + pairs, pairs), 4)

    local_waits = {}
    for i, (q, s) in enumerate(slots):
        col = pl.ds(pl.multiple_of(dp_dev(s) * hs + q * chunk, 128), chunk)
        local_waits["g", q, s] = start(pltpu.make_async_copy(gate_hbm.at[0, :, col], gate_v.at[i], gate_sem.at[i]))
        local_waits["u", q, s] = start(pltpu.make_async_copy(up_hbm.at[0, :, col], up_v.at[i], up_sem.at[i]))
    own = pl.ds(pl.multiple_of(me_e * sh, 128), sh)
    local_waits["sg"] = start(pltpu.make_async_copy(sg_hbm.at[:, own], sg_v, shw_sem.at[0]))
    local_waits["su"] = start(pltpu.make_async_copy(su_hbm.at[:, own], su_v, shw_sem.at[1]))
    local_waits["sd"] = start(pltpu.make_async_copy(sd_hbm.at[own, :], sd_v, shw_sem.at[2]))
    for i, (q, s) in enumerate(slots):
        row = pl.ds(pl.multiple_of(dp_src(s) * hs + q * chunk, 128), chunk)
        local_waits["d", q, s] = start(pltpu.make_async_copy(down_hbm.at[0, row, :], down_v.at[i], down_sem.at[i]))

    barrier = pltpu.get_barrier_semaphore()
    for s in range(1, n_dp):
        pl.semaphore_signal(barrier, inc=1, device_id=(dp_dev(s), me_e), device_id_type=MESH)
    for s in range(1, zs):
        pl.semaphore_signal(barrier, inc=1, device_id=(me_d, z_dev(s)), device_id_type=MESH)
    pl.semaphore_signal(barrier, inc=1, device_id=(me_d, partner), device_id_type=MESH)

    top = ids_ref.shape[0]
    flip[...] = jnp.zeros_like(flip)
    flip[:top, :tokens] = ids_ref[...].astype(F32)
    flip[top:2 * top, :tokens] = w_ref[...]
    named_ids = lax.broadcasted_iota(jnp.int32, (128, 128), 0).astype(F32)
    table = jnp.zeros((128, 128), F32)
    for k in range(top):
        table += jnp.where(flip[k:k + 1, :] == named_ids, flip[top + k:top + k + 1, :], 0.0)
    mine = jnp.transpose(table)[:tokens]
    m_own[...] = mine
    m_all[me_e] = mine
    x_all[me_e] = x_ref[...]
    c_all[me_e] = cur_ref[...]
    pl.semaphore_wait(barrier, n_dp - 1 + zs - 1 + 1)

    sends = []

    def remote(src, dst, ssem, rsem, dp, e):
        copy = pltpu.make_async_remote_copy(
            src_ref=src, dst_ref=dst, send_sem=ssem, recv_sem=rsem, device_id=(dp, e), device_id_type=MESH
        )
        copy.start()
        sends.append(copy)

    def arrived(dst, ssem, rsem):
        pltpu.make_async_remote_copy(
            src_ref=dst, dst_ref=dst, send_sem=ssem, recv_sem=rsem, device_id=(me_d, partner), device_id_type=MESH
        ).wait_recv()

    groups = [(m_own, m_all, m_s, m_r, mp_s, mp_r), (x_ref, x_all, x_s, x_r, xp_s, xp_r), (cur_ref, c_all, c_s, c_r, cp_s, cp_r)]

    def spread(src, buf, ss, rr, ps, pr):
        remote(src, buf.at[me_e], ps.at[0], pr.at[0], me_d, partner)
        for s in range(1, zs):
            remote(src, buf.at[me_e], ss.at[s], rr.at[s], me_d, z_dev(s))

    def relay(s, src, buf, ss, rr, ps, pr):
        if s:
            block = buf.at[z_src(s)]
            arrived(block, ss.at[s], rr.at[s])
            remote(block, block, ps.at[s], pr.at[s], me_d, partner)

    def collect(s, src, buf, ss, rr, ps, pr):
        arrived(buf.at[z_src(s) + 1 - 2 * c], ps.at[s], pr.at[s])

    spread(*groups[0])
    spread(*groups[1])
    spread(*groups[2])
    held = 4 * tokens
    below = lax.broadcasted_iota(jnp.int32, (held, held), 1) < lax.broadcasted_iota(jnp.int32, (held, held), 0)
    below = jnp.where(below, 1.0, 0.0).astype(BF)
    pick = lax.broadcasted_iota(jnp.int32, (held, 128), 1) == me_e
    padded = -(-rows // 128) * 128
    slot = lax.broadcasted_iota(jnp.int32, (held, padded), 1).astype(F32)
    combine = []
    for a in range(pairs):
        for s in (2 * a, 2 * a + 1):
            relay(s, *groups[0])
        for s in (2 * a, 2 * a + 1):
            relay(s, *groups[1])
        for s in (2 * a, 2 * a + 1):
            collect(s, *groups[0])
        routing = m_all[group_blocks(a)].reshape(held, 128)
        rank = dot(below, jnp.where(routing > 0, 1.0, 0.0).astype(BF))
        rank_col = jnp.sum(jnp.where(pick, rank, 0.0), axis=1, keepdims=True)
        scale_col = jnp.sum(jnp.where(pick, routing, 0.0), axis=1, keepdims=True)
        placed_t = jnp.where(jnp.logical_and(slot == rank_col, scale_col > 0), 1.0, 0.0)
        gather = jnp.transpose(placed_t)[:rows].astype(BF)
        combine.append((placed_t.astype(BF)[:, :rows], scale_col))
        for s in (2 * a, 2 * a + 1):
            collect(s, *groups[1])
        xc[a] = dot(gather, x_all[group_blocks(a)].reshape(held, width)).astype(BF)
        for i, (q, s) in enumerate(slots):
            if a == 0:
                local_waits["g", q, s].wait()
                local_waits["u", q, s].wait()
            n = a * len(slots) + i
            part[n, :, :chunk] = dot(xc[a], gate_v[i]).astype(BF)
            part[n, :, chunk:] = dot(xc[a], up_v[i]).astype(BF)
            if s:
                remote(part.at[n], rs_in.at[n], rs_s.at[n], rs_r.at[n], dp_dev(s), me_e)

    def act(term, n):
        gate, upper = term[:, :n], term[:, n:]
        return (gate / (1.0 + jnp.exp(-gate)) * upper).astype(BF)

    def routed_act(a, q):
        base = a * len(slots) + q * n_dp
        term = part[base + n_dp - 1].astype(F32)
        for s in range(1, n_dp):
            i = base + s - 1
            arrived(rs_in.at[i], rs_s.at[i], rs_r.at[i])
            term = term + rs_in[i].astype(F32)
        j = base + n_dp - 1
        hid[j] = act(term, chunk)
        for s in range(1, n_dp):
            i = base + s - 1
            remote(hid.at[j], hid.at[i], hid_s.at[i], hid_r.at[i], dp_dev(s), me_e)

    def routed_down(a):
        for q in range(PARTS):
            base = q * n_dp
            for s in [0, *range(1, n_dp)]:
                i = base + (s - 1 if s else n_dp - 1)
                n = a * len(slots) + i
                if s:
                    arrived(hid.at[n], hid_s.at[n], hid_r.at[n])
                if a == pairs - 1:
                    local_waits["d", q, s].wait()
                value = dot(hid[n], down_v[i])
                acc[...] = value if q == 0 and s == 0 else acc[...] + value

    for s in range(1, zs):
        relay(s, *groups[2])
    for s in range(zs):
        collect(s, *groups[2])
    local_waits["sg"].wait()
    local_waits["su"].wait()
    cur = c_all[...].reshape(total, width)
    sh_part[:, :, :sh] = dot(cur, sg_v[...]).astype(BF).reshape(n_dp, share, sh)
    sh_part[:, :, sh:] = dot(cur, su_v[...]).astype(BF).reshape(n_dp, share, sh)
    for s in range(1, n_dp):
        remote(sh_part.at[dp_dev(s)], sh_in.at[s], shp_s.at[s], shp_r.at[s], dp_dev(s), me_e)
    for q in range(PARTS):
        routed_act(pairs - 1, q)
    term = sh_part[me_d].astype(F32)
    for s in range(1, n_dp):
        arrived(sh_in.at[s], shp_s.at[s], shp_r.at[s])
        term = term + sh_in[s].astype(F32)
    sh_hid[me_d] = act(term, sh)
    for s in range(1, n_dp):
        remote(sh_hid.at[me_d], sh_hid.at[me_d], shh_s.at[s], shh_r.at[s], dp_dev(s), me_e)

    for a in range(pairs - 2, -1, -1):
        for q in range(PARTS):
            routed_act(a, q)
    for a in range(pairs - 1, -1, -1):
        routed_down(a)
        if a == pairs - 1:
            for s in range(1, n_dp):
                arrived(sh_hid.at[dp_src(s)], shh_s.at[s], shh_r.at[s])
            local_waits["sd"].wait()
            shv[...] = dot(sh_hid[...].reshape(total, sh), sd_v[...]).reshape(n_e, tokens, width)
        scatter, scale_col = combine[a]
        value = scale_col * dot(scatter, acc[...].astype(BF))
        value = value + shv[group_blocks(a)].reshape(held, width)
        contrib[group_blocks(a)] = value.astype(BF).reshape(4, tokens, width)
        for s in (2 * a + 1, 2 * a):
            remote(contrib.at[z_src(s) + 1 - 2 * c], pair_in.at[s], pair_s.at[s], pair_r.at[s], me_d, partner)
        for s in (2 * a + 1, 2 * a):
            arrived(pair_in.at[s], pair_s.at[s], pair_r.at[s])
            summed = contrib[z_src(s)].astype(F32) + pair_in[s].astype(F32)
            if s:
                fin_out[s] = summed.astype(BF)
                remote(fin_out.at[s], fin_in.at[s], fin_s.at[s], fin_r.at[s], me_d, z_src(s))
            else:
                own_sum[...] = summed
    both = own_sum[...]
    for s in range(1, zs):
        arrived(fin_in.at[s], fin_s.at[s], fin_r.at[s])
        both = both + fin_in[s].astype(F32)
    out_ref[...] = both.astype(BF)
    for copy in sends:
        copy.wait_send()


def fused(n_dp, n_e, shortcut_in, current_in, expert_ids, route_weight, gate_weight, up_weight, down_weight, shared_gate, shared_up, shared_down):
    tokens, width = shortcut_in.shape
    hidden = gate_weight.shape[2]
    top = expert_ids.shape[1]
    capacity = 3 * tokens * top // (2 * n_e)
    rows = min(-(-capacity * 4 // 16) * 16, 4 * tokens)
    chunk = hidden // n_dp // PARTS
    count = PARTS * n_dp
    sh = hidden // n_e
    zs = n_e // 2
    pairs = zs // 2
    total = n_e * tokens
    share = total // n_dp
    V = pltpu.VMEM
    S = pltpu.SemaphoreType.DMA
    scratch = [
        V((count, width, chunk), BF), V((count, width, chunk), BF), V((count, chunk, width), BF),
        V((width, sh), BF), V((width, sh), BF), V((sh, width), BF),
        V((-(-2 * top // 8) * 8, 128), F32), V((tokens, 128), F32), V((n_e, tokens, 128), F32), V((n_e, tokens, width), BF), V((n_e, tokens, width), BF),
        V((pairs, rows, width), BF), V((pairs * count, rows, 2 * chunk), BF), V((pairs * count, rows, 2 * chunk), BF),
        V((pairs * count, rows, chunk), BF), V((rows, width), F32), V((n_e, tokens, width), F32),
        V((n_dp, share, 2 * sh), BF), V((n_dp, share, 2 * sh), BF), V((n_dp, share, sh), BF), V((tokens, width), F32),
        V((n_e, tokens, width), BF), V((zs, tokens, width), BF), V((zs, tokens, width), BF), V((zs, tokens, width), BF),
        S((count,)), S((count,)), S((count,)), S((3,)),
        *[S((zs,)) for _ in range(12)],
        *[S((pairs * count,)) for _ in range(4)],
        *[S((n_dp,)) for _ in range(4)],
        *[S((zs,)) for _ in range(4)],
    ]
    vm = pl.BlockSpec(memory_space=pltpu.VMEM)
    hbm = pl.BlockSpec(memory_space=pl.ANY)
    return pl.pallas_call(
        functools.partial(layer_kernel, n_dp, n_e, rows),
        out_shape=jax.ShapeDtypeStruct((tokens, width), BF),
        in_specs=[vm] * 4 + [hbm] * 6,
        out_specs=vm,
        scratch_shapes=scratch,
        compiler_params=pltpu.CompilerParams(collective_id=0, has_side_effects=True, vmem_limit_bytes=60 * 1024 * 1024),
    )(shortcut_in, current_in, expert_ids.T, route_weight.T, gate_weight, up_weight, down_weight, shared_gate, shared_up, shared_down)


def body(n_dp, n_e, *arrays):
    tokens, width = arrays[0].shape
    experts, _, hidden = arrays[4].shape
    aligned = (
        experts == 1 and n_e % 4 == 0 and tokens <= 128 and n_e <= 128 and tokens % 16 == 0 and width % 128 == 0
        and hidden % (n_dp * PARTS * 128) == 0 and hidden % (n_e * 128) == 0
        and n_e * tokens % (n_dp * 16) == 0
    )
    return fused(n_dp, n_e, *arrays) if aligned else local(*arrays)


def solution(mesh):
    placed = (
        P("expert", "dp"),
        P("expert", "dp"),
        P("expert", None),
        P("expert", None),
        P("expert", "dp", None),
        P("expert", "dp", None),
        P("expert", None, "dp"),
        P("dp", None),
        P("dp", None),
        P(None, "dp"),
    )
    return jax.shard_map(
        functools.partial(body, mesh.shape["dp"], mesh.shape["expert"]), mesh=mesh, in_specs=placed, out_specs=P("expert", "dp"), check_vma=False
    )
```

profile of v0, /device:TPU:0, one launch (start us, length us, event | category | flops | bytes accessed | tf_op | source)
XLA Modules:
  0.0 42.2 jit_solution(7038945323196627476)
XLA Ops:
  0.0 40.8 %shard_map.100 = bf16[16,1792]{1,0:T(8,128)(2,1)} custom-call(bf16[16,1792]{1,0:T(8,128)(2,1)} %x_ref.1, bf16[16,1792]{1,0:T(8,128)(2,1)} %cur_ref.1, s32[4,16]{1,0:T(4,128)} %bitcast.2, f32[4,16]{1,0:T(4,128)} %bitcast.3, bf16[1,1792,2048]{2,1,0:T(8,128)(2,1)} %gate_hbm.1, bf16[1,1792,2048]{2,1,0:T(8,128)(2,1)} %up_hbm.1, bf16[1,2048,1792]{2,1,0:T(8,128)(2,1)} %down_hbm.1, ...), custom_call_target="tpu_custom_call" | custom-call | tf_op jit(solution)/shard_map/pallas_call | solution.py:358
  40.8 1.4 %copy.12 = bf16[16,1792]{1,0:T(8,128)(2,1)} copy(bf16[16,1792]{1,0:T(8,128)(2,1)} %shard_map.100) | data formatting | bytes 114688
where the time goes:
time: 42.4 us; the launch traced here: 42.2 us
  Pallas kernels  40.8 us (96%)
  local copies, waits for them, and re-layouts  1.45 us (3%)
    pallas_call x1, Pallas kernels, fused(): pl.pallas_call(functools.partial(layer_kernel, n_dp, n_e, rows), out_shap...  40.8 us
    unnamed x1, local copies, waits for them, and re-layouts  1.45 us

commit v1 on v0

v1 whole, which is shorter than its diff:
```python
import functools

import jax
import jax.numpy as jnp
from jax import lax
from jax.experimental import pallas as pl
from jax.experimental.pallas import tpu as pltpu
from jax.sharding import PartitionSpec as P


def activate(summed):
    return (jax.nn.silu(summed[:, 0]) * summed[:, 1]).astype(jnp.bfloat16)


def hidden_of(partial_value):
    summed = lax.psum_scatter(
        partial_value.astype(jnp.bfloat16), "dp", scatter_dimension=2, tiled=True
    ).astype(jnp.float32)
    return lax.all_gather(activate(summed), "dp", axis=1, tiled=True)


def send_rows(outgoing):
    return lax.all_to_all(outgoing, "expert", split_axis=0, concat_axis=0, tiled=True)


def expert_partial(arrived, gate_weight, up_weight):
    gate = jnp.einsum("sacd,adh->sach", arrived, gate_weight, preferred_element_type=jnp.float32)
    upper = jnp.einsum("sacd,adh->sach", arrived, up_weight, preferred_element_type=jnp.float32)
    stacked = jnp.stack([gate, upper], axis=3)
    return stacked.reshape(-1, 2, gate_weight.shape[2])


def local(
    shortcut_in,
    current_in,
    expert_ids,
    route_weight,
    gate_weight,
    up_weight,
    down_weight,
    shared_gate,
    shared_up,
    shared_down,
):
    sources = lax.axis_size("expert")
    local_experts = gate_weight.shape[0]
    experts = sources * local_experts
    tokens, top = expert_ids.shape
    capacity = 3 * tokens * top // (2 * experts)
    width = shortcut_in.shape[1]
    hidden_units = gate_weight.shape[2]
    flat_ids = expert_ids.reshape(-1)
    onehot = (flat_ids[:, None] == jnp.arange(experts, dtype=jnp.int32)[None, :]).astype(jnp.int32)
    rank = jnp.sum((jnp.cumsum(onehot, axis=0) - 1) * onehot, axis=1)
    slot = (flat_ids * capacity + rank).reshape(tokens, top)
    positions = jnp.arange(experts * capacity, dtype=jnp.int32)
    place = jnp.sum((slot[None, :, :] == positions[:, None, None]).astype(jnp.bfloat16), axis=2)
    outgoing = jnp.dot(place, shortcut_in, preferred_element_type=jnp.float32).astype(jnp.bfloat16)
    outgoing = outgoing.reshape(sources, local_experts * capacity, width)
    shared_gate_sum = jnp.dot(current_in, shared_gate, preferred_element_type=jnp.float32)
    shared_up_sum = jnp.dot(current_in, shared_up, preferred_element_type=jnp.float32)
    shared_partial = jnp.stack([shared_gate_sum, shared_up_sum], axis=1)
    routed_rows = experts * capacity
    arrived = send_rows(outgoing).reshape(sources, local_experts, capacity, width)
    routed_partial = expert_partial(arrived, gate_weight, up_weight)
    joined = hidden_of(jnp.concatenate([routed_partial, shared_partial], axis=0))
    routed_hidden = joined[:routed_rows]
    shared_hidden = joined[routed_rows:]
    routed_hidden = routed_hidden.reshape(sources, local_experts, capacity, hidden_units)
    expert_out = jnp.einsum(
        "sach,ahd->sacd", routed_hidden, down_weight, preferred_element_type=jnp.float32
    ).astype(jnp.bfloat16)
    returned = lax.all_to_all(
        expert_out.reshape(sources, local_experts * capacity, width),
        "expert",
        split_axis=0,
        concat_axis=0,
        tiled=True,
    )
    picked = returned.reshape(routed_rows, width)[slot]
    routed = jnp.sum(route_weight[:, :, None] * picked.astype(jnp.float32), axis=1)
    shared_out = jnp.dot(shared_hidden, shared_down, preferred_element_type=jnp.float32)
    return (shared_out + routed).astype(jnp.bfloat16)


MESH = pl.DeviceIdType.MESH
BF = jnp.bfloat16
F32 = jnp.float32
PARTS = 2


def dot(a, b):
    return jnp.dot(a, b, preferred_element_type=F32)


def layer_kernel(
    n_dp, n_e, cap, groups, near,
    x_hbm, cur_hbm, ids_hbm, w_hbm, gate_hbm, up_hbm, down_hbm, sg_hbm, su_hbm, sd_hbm,
    out_ref,
    gu_v, down_v, sgu_v, sd_v, ids_v, w_v, flip, xm, cm,
    xc, part, rs_in, hid, acc, shv, sh_part, sh_in, sh_hid, own_sum, contrib, pair_in, fin_out, fin_in,
    in_sem, gu_sem, down_sem, shw_sem,
    snd, x_r, xp_r, c_r, cp_r, rs_s, rs_r, hid_s, hid_r, shp_r, shh_r, pair_r, fin_r,
):
    me_d = lax.axis_index("dp")
    me_e = lax.axis_index("expert")
    zs = n_e // 2
    z, c = me_e // 2, lax.rem(me_e, 2)
    pairs = zs // 2
    p, b = z // 2, lax.rem(z, 2)
    partner = 2 * z + (1 - c)
    tokens, width = x_hbm.shape
    top = ids_hbm.shape[0]
    chunk = gu_v.shape[2] // 2
    hs = chunk * PARTS
    shc = sgu_v.shape[1] // 2
    held = 2 * tokens
    slots = [(q, s) for q in range(PARTS) for s in [*range(n_dp - 1, 0, -1), 0]]

    def start(src, dst, sem):
        copy = pltpu.make_async_copy(src, dst, sem)
        copy.start()
        return copy

    def landed(dst, sem):
        pltpu.make_async_copy(dst, dst, sem).wait()

    ys = n_dp // 2
    y, x = me_d // 2, lax.rem(me_d, 2)
    to_dp = [2 * lax.rem(y + s // 2, ys) + lax.rem(x + s % 2, 2) for s in range(n_dp)]
    from_dp = [2 * lax.rem(y - s // 2 + ys, ys) + lax.rem(x + s % 2, 2) for s in range(n_dp)]
    to_z = [2 * (2 * lax.rem(p + s // 2, pairs) + lax.rem(b + s % 2, 2)) + c for s in range(zs)]
    from_z = [2 * (2 * lax.rem(p - s // 2 + pairs, pairs) + lax.rem(b + s % 2, 2)) + c for s in range(zs)]

    def dp_dev(s):
        return to_dp[s]

    def dp_src(s):
        return from_dp[s]

    def z_dev(s):
        return to_z[s]

    def z_src(s):
        return from_z[s]

    barrier = pltpu.get_barrier_semaphore()
    pl.semaphore_signal(barrier, inc=1, device_id=(me_d, partner), device_id_type=MESH)
    for s in range(1, zs):
        pl.semaphore_signal(barrier, inc=1, device_id=(me_d, z_dev(s)), device_id_type=MESH)
    for s in range(1, n_dp):
        pl.semaphore_signal(barrier, inc=1, device_id=(dp_dev(s), me_e), device_id_type=MESH)

    got_ids = start(ids_hbm, ids_v, in_sem.at[0])
    got_w = start(w_hbm, w_v, in_sem.at[1])
    got_x = start(x_hbm, xm.at[c, :, pl.ds(0, width)], in_sem.at[2])
    got_cur = start(cur_hbm, cm.at[c], in_sem.at[3])
    def fetch_shared():
        mine = pl.ds(pl.multiple_of(lax.rem(me_e, 2 * near) * shc, 128), shc)
        start(sg_hbm.at[:, mine], sgu_v.at[:, pl.ds(0, shc)], shw_sem.at[0])
        start(su_hbm.at[:, mine], sgu_v.at[:, pl.ds(shc, shc)], shw_sem.at[0])
        start(sd_hbm.at[mine, :], sd_v, shw_sem.at[1])

    def fetch_down():
        for q in range(PARTS):
            for i, s in enumerate([*range(n_dp - 1, 0, -1), 0]):
                row = pl.ds(pl.multiple_of(dp_src(s) * hs + q * chunk, 128), chunk)
                start(down_hbm.at[0, row, :], down_v.at[pl.ds((q * n_dp + i) * chunk, chunk), :], down_sem.at[q])

    def remote(src, dst, ssem, rsem, dp, e):
        pltpu.make_async_remote_copy(
            src_ref=src, dst_ref=dst, send_sem=ssem, recv_sem=rsem, device_id=(dp, e), device_id_type=MESH
        ).start()

    before = lax.broadcasted_iota(jnp.int32, (128, 128), 0) < lax.broadcasted_iota(jnp.int32, (128, 128), 1)
    before = jnp.where(before, 1.0, 0.0).astype(BF)
    flip[...] = jnp.zeros_like(flip)
    got_ids.wait()
    got_w.wait()
    flip[:top, :tokens] = ids_v[...].astype(F32)
    flip[top:2 * top, :tokens] = w_v[...]
    named = flip[...]
    named = jnp.where(c == 1, pltpu.roll(named, tokens, 1), named)
    flip[...] = named
    exact = flip[top:2 * top, :]
    first = exact.astype(BF).astype(F32)
    second = (exact - first).astype(BF).astype(F32)
    flip[top:2 * top, :] = first
    flip[2 * top:3 * top, :] = second
    flip[3 * top:4 * top, :] = exact - first - second
    xm[c, :, width:] = flip[...].astype(BF)
    got_x.wait()
    got_cur.wait()
    for i, (q, s) in enumerate(slots):
        col = pl.ds(pl.multiple_of(dp_dev(s) * hs + q * chunk, 128), chunk)
        start(gate_hbm.at[0, :, col], gu_v.at[i, :, pl.ds(0, chunk)], gu_sem.at[i])
        start(up_hbm.at[0, :, col], gu_v.at[i, :, pl.ds(chunk, chunk)], gu_sem.at[i])
    with jax.named_scope("barrier"):
        pl.semaphore_wait(barrier, n_dp - 1 + zs - 1 + 1)

    remote(xm.at[c], xm.at[c], snd.at[0], xp_r.at[0], me_d, partner)
    for s in range(1, zs):
        remote(xm.at[c], xm.at[2 * s + c], snd.at[0], x_r.at[s], me_d, z_dev(s))
    remote(cm.at[c], cm.at[c], snd.at[1], cp_r.at[0], me_d, partner)
    for s in range(1, near):
        remote(cm.at[c], cm.at[2 * s + c], snd.at[1], c_r.at[s], me_d, z_dev(s))

    def relay_x(s):
        with jax.named_scope(f"relay{s}"):
            landed(xm.at[2 * s + c], x_r.at[s])
        remote(xm.at[2 * s + c], xm.at[2 * s + c], snd.at[0], xp_r.at[s], me_d, partner)

    def relay_cur(s):
        with jax.named_scope(f"crelay{s}"):
            landed(cm.at[2 * s + c], c_r.at[s])
        remote(cm.at[2 * s + c], cm.at[2 * s + c], snd.at[1], cp_r.at[s], me_d, partner)

    me_f = me_e.astype(F32)

    def chosen(block):
        table = xm[block, :, width:].astype(F32)
        weight = table[top:2 * top] + table[2 * top:3 * top] + table[3 * top:4 * top]
        return jnp.sum(jnp.where(table[:top] == me_f, weight, 0.0), axis=0, keepdims=True)

    def route(g):
        rows = part[g].shape[1]
        padded = -(-rows // 16) * 16
        for s in groups[g]:
            with jax.named_scope(f"coll{s}"):
                landed(xm.at[2 * s + 1 - c], xp_r.at[s])
        scale = None
        for k, s in enumerate(groups[g]):
            one = chosen(2 * s) + chosen(2 * s + 1)
            one = pltpu.roll(one, held * k, 1) if k else one
            scale = one if scale is None else scale + one
        scale = jnp.broadcast_to(scale, (8, 128))
        rank = dot(jnp.where(scale > 0, 1.0, 0.0).astype(BF), before)[:1]
        scale = scale[:1]
        place = lax.broadcasted_iota(jnp.int32, (padded, 128), 0).astype(F32)
        place = jnp.where(jnp.logical_and(place == rank, scale > 0), 1.0, 0.0)
        size = held * len(groups[g])
        source = jnp.concatenate([xm[2 * s:2 * s + 2, :, :width].reshape(held, width) for s in groups[g]], axis=0)
        xc[g][...] = dot(place[:, :size].astype(BF), source).astype(BF)
        return place, scale

    def gate_up(g, hooks):
        rows = part[g].shape[1]
        for i, (q, s) in enumerate(slots):
            if g == 0:
                with jax.named_scope(f"w{i}"):
                    landed(gu_v.at[i], gu_sem.at[i])
            part[g][i] = dot(xc[g][...], gu_v[i])[:rows].astype(BF)
            if s:
                remote(part[g].at[i], rs_in[g].at[i], rs_s.at[g], rs_r.at[PARTS * g + q], dp_dev(s), me_e)
            for hook in hooks.get(i, ()):
                hook()

    def back(g, place, scale):
        rows = part[g].shape[1]
        size = held * len(groups[g])
        tall = jnp.concatenate([place, jnp.zeros((128 - place.shape[0], 128), F32)], axis=0)
        turned = jnp.transpose(tall)[:size]
        weight = jnp.sum(place * scale, axis=1, keepdims=True)[:rows]
        return turned[:, :rows].astype(BF), weight

    def gated(term, n):
        gate, upper = term[:, :n], term[:, n:]
        return (gate / (1.0 + jnp.exp(-gate)) * upper).astype(BF)

    def act(g, q):
        base = q * n_dp
        others = pl.ds(base, n_dp - 1)
        with jax.named_scope(f"rs{g}{q}"):
            landed(rs_in[g].at[others], rs_r.at[PARTS * g + q])
        term = part[g][base + n_dp - 1].astype(F32)
        for s in range(1, n_dp):
            term = term + rs_in[g][base + n_dp - 1 - s].astype(F32)
        own = base + n_dp - 1
        hid[g][own] = gated(term, chunk)
        for s in range(1, n_dp):
            remote(hid[g].at[own], hid[g].at[base + n_dp - 1 - s], hid_s.at[g], hid_r.at[PARTS * g + q], dp_dev(s), me_e)

    def down(g, weight, between=None):
        span = n_dp * chunk

        def gathered(q):
            with jax.named_scope(f"hid{g}{q}"):
                landed(hid[g].at[pl.ds(q * n_dp, n_dp - 1)], hid_r.at[PARTS * g + q])
            if g == 0:
                landed(down_v.at[pl.ds(q * span, span), :], down_sem.at[q])
            return [hid[g][q * n_dp + i] for i in range(n_dp)]

        rows = part[g].shape[1]
        if between is not None:
            for q in range(PARTS):
                value = dot(jnp.concatenate(gathered(q), axis=1), down_v[q * span:(q + 1) * span])
                if q < PARTS - 1:
                    acc[:rows] = value if q == 0 else acc[:rows] + value
                    between()
            value = acc[:rows] + value
        else:
            pieces = [piece for q in range(PARTS) for piece in gathered(q)]
            value = dot(jnp.concatenate(pieces, axis=1), down_v[...])
        return (weight * value).astype(BF)

    def give(g, turned, value):
        value = dot(turned, value)
        for k, s in enumerate(groups[g]):
            one = value[k * held:(k + 1) * held].reshape(2, tokens, width)
            if s < near:
                one = one + shv[2 * s:2 * s + 2]
            contrib[s] = one.astype(BF)
            remote(contrib.at[s, 1 - c], pair_in.at[s], snd.at[4], pair_r.at[s], me_d, partner)

    def settle(s):
        with jax.named_scope(f"pair{s}"):
            landed(pair_in.at[s], pair_r.at[s])
        summed = contrib[s, c].astype(F32) + pair_in[s].astype(F32)
        if s:
            fin_out[s - 1] = summed.astype(BF)
            remote(fin_out.at[s - 1], fin_in.at[s - 1], snd.at[5], fin_r.at[s], me_d, z_src(s))
        else:
            own_sum[...] = summed

    def shared_up():
        for s in range(near):
            with jax.named_scope(f"ccoll{s}"):
                landed(cm.at[2 * s + 1 - c], cp_r.at[s])
        with jax.named_scope("shw"):
            landed(sgu_v, shw_sem.at[0])
        cur = cm[...].reshape(near * held, width)
        sh_part[...] = dot(cur, sgu_v[...]).astype(BF).reshape(sh_part.shape)
        for s in range(1, n_dp):
            remote(sh_part.at[dp_dev(s)], sh_in.at[s - 1], snd.at[2], shp_r.at[0], dp_dev(s), me_e)

    def shared_act():
        with jax.named_scope("shrs"):
            landed(sh_in, shp_r.at[0])
        term = sh_part[me_d].astype(F32)
        for s in range(1, n_dp):
            term = term + sh_in[s - 1].astype(F32)
        sh_hid[me_d] = gated(term, shc)
        for s in range(1, n_dp):
            remote(sh_hid.at[me_d], sh_hid.at[me_d], snd.at[3], shh_r.at[s], dp_dev(s), me_e)

    def shared_down():
        for s in range(1, n_dp):
            with jax.named_scope(f"shh{s}"):
                landed(sh_hid.at[dp_src(s)], shh_r.at[s])
        landed(sd_v, shw_sem.at[1])
        shv[...] = dot(sh_hid[...].reshape(near * held, shc), sd_v[...]).reshape(shv.shape)

    order = list(range(len(groups)))
    kept = {}

    def do(*calls):
        return [functools.partial(*call) for call in calls]

    hooks = [
        {2: do((fetch_shared,)), 4: do((fetch_down,)), 6: do((relay_x, 1))},
        {2: do((act, 0, 0)), 4: do((act, 0, 1), (relay_x, 2)), 5: do((relay_cur, 1)), 6: do((relay_x, 3))},
        {},
    ]
    for g in order:
        place, scale = route(g)
        gate_up(g, hooks[g])
        kept[g] = back(g, place, scale)
        if g == 1:
            shared_up()
    for q in range(PARTS):
        act(1, q)
    shared_act()
    first_value = down(0, kept[0][1])
    act(2, 0)
    act(2, 1)
    second_value = down(1, kept[1][1])
    shared_down()
    give(0, kept[0][0], first_value)
    give(1, kept[1][0], second_value)

    def near_home():
        settle(1)
        settle(0)

    give(2, kept[2][0], down(2, kept[2][1], near_home))
    settle(3)
    settle(2)
    both = own_sum[...]
    for s in range(1, zs):
        with jax.named_scope(f"fin{s}"):
            landed(fin_in.at[s - 1], fin_r.at[s])
        both = both + fin_in[s - 1].astype(F32)
    out_ref[...] = both.astype(BF)

    def sent(ref, sem):
        pltpu.make_async_remote_copy(
            src_ref=ref, dst_ref=ref, send_sem=sem, recv_sem=sem, device_id=(me_d, partner), device_id_type=MESH
        ).wait_send()

    with jax.named_scope("sendwait"):
        sent(xm.at[pl.ds(0, 2 * zs - 1)], snd.at[0])
        sent(cm.at[pl.ds(0, 2 * near - 1)], snd.at[1])
        sent(sh_part.at[pl.ds(0, n_dp - 1)], snd.at[2])
        sent(sh_hid.at[pl.ds(0, n_dp - 1)], snd.at[3])
        sent(pair_in, snd.at[4])
        sent(fin_out, snd.at[5])
        for g in order:
            sent(part[g].at[pl.ds(0, PARTS * (n_dp - 1))], rs_s.at[g])
            sent(hid[g].at[pl.ds(0, PARTS * (n_dp - 1))], hid_s.at[g])


GROUPS = ((0,), (1,), (2, 3))
NEAR = 2


def fused(n_dp, n_e, shortcut_in, current_in, expert_ids, route_weight, gate_weight, up_weight, down_weight, shared_gate, shared_up, shared_down):
    tokens, width = shortcut_in.shape
    hidden = gate_weight.shape[2]
    top = expert_ids.shape[1]
    cap = 3 * tokens * top // (2 * n_e)
    chunk = hidden // n_dp // PARTS
    count = PARTS * n_dp
    zs = n_e // 2
    shc = hidden // (2 * NEAR)
    share = 2 * NEAR * tokens // n_dp
    rows = [2 * cap * len(g) for g in GROUPS]
    n_g = len(GROUPS)
    V = pltpu.VMEM
    S = pltpu.SemaphoreType.DMA
    scratch = [
        V((count, width, 2 * chunk), BF), V((hidden, width), BF), V((width, 2 * shc), BF), V((shc, width), BF),
        V((top, tokens), jnp.int32), V((top, tokens), F32), V((tokens, 128), F32),
        V((n_e, tokens, width + 128), BF), V((2 * NEAR, tokens, width), BF),
        [V((-(-r // 16) * 16, width), BF) for r in rows], [V((count, r, 2 * chunk), BF) for r in rows], [V((count, r, 2 * chunk), BF) for r in rows], [V((count, r, chunk), BF) for r in rows],
        V((max(rows), width), F32), V((2 * NEAR, tokens, width), F32),
        V((n_dp, share, 2 * shc), BF), V((n_dp - 1, share, 2 * shc), BF), V((n_dp, share, shc), BF), V((tokens, width), F32),
        V((zs, 2, tokens, width), BF), V((zs, tokens, width), BF), V((zs - 1, tokens, width), BF), V((zs - 1, tokens, width), BF),
        S((4,)), S((count,)), S((PARTS,)), S((2,)),
        S((6,)), S((zs,)), S((zs,)), S((NEAR,)), S((NEAR,)),
        S((n_g,)), S((PARTS * n_g,)), S((n_g,)), S((PARTS * n_g,)), S((1,)), S((n_dp,)), S((zs,)), S((zs,)),
    ]
    vm = pl.BlockSpec(memory_space=pltpu.VMEM)
    hbm = pl.BlockSpec(memory_space=pl.ANY)
    return pl.pallas_call(
        functools.partial(layer_kernel, n_dp, n_e, cap, GROUPS, NEAR),
        out_shape=pltpu.VMEM((tokens, width), BF),
        in_specs=[hbm] * 10,
        out_specs=vm,
        scratch_shapes=scratch,
        compiler_params=pltpu.CompilerParams(collective_id=0, has_side_effects=True, vmem_limit_bytes=60 * 1024 * 1024),
    )(shortcut_in, current_in, expert_ids.T, route_weight.T, gate_weight, up_weight, down_weight, shared_gate, shared_up, shared_down)


def body(n_dp, n_e, *arrays):
    tokens, width = arrays[0].shape
    top = arrays[2].shape[1]
    experts, _, hidden = arrays[4].shape
    aligned = (
        experts == 1 and n_e == 2 * sum(len(g) for g in GROUPS) and 4 * top <= tokens and tokens == 16 and width % 128 == 0
        and hidden % (n_dp * PARTS * 128) == 0 and hidden % (2 * NEAR * 128) == 0
        and 2 * NEAR * tokens % (n_dp * 16) == 0 and 3 * tokens * top % (2 * n_e) == 0 and 2 * (3 * tokens * top // (2 * n_e)) % 8 == 0
    )
    return fused(n_dp, n_e, *arrays) if aligned else local(*arrays)


def solution(mesh):
    placed = (
        P("expert", "dp"),
        P("expert", "dp"),
        P("expert", None),
        P("expert", None),
        P("expert", "dp", None),
        P("expert", "dp", None),
        P("expert", None, "dp"),
        P("dp", None),
        P("dp", None),
        P(None, "dp"),
    )
    return jax.shard_map(
        functools.partial(body, mesh.shape["dp"], mesh.shape["expert"]), mesh=mesh, in_specs=placed, out_specs=P("expert", "dp"), check_vma=False
    )
```

time: 42.4 us -> 38.4 us (0.906)
  Pallas kernels: 40.8 us -> 37.6 us
  local copies, waits for them, and re-layouts: 1.45 us -> 0.63 us
    pallas_call x1, Pallas kernels: 40.8 us -> 37.6 us  [fused(): pl.pallas_call(functools.partial(layer_kernel, n_dp, n_e, cap, GROUPS, NE...]
    unnamed x1, local copies, waits for them, and re-layouts: 1.45 us -> 0.63 us
where the time goes in v1:
time: 38.4 us; the launch traced here: 38.2 us
  Pallas kernels  37.6 us (98%)
  local copies, waits for them, and re-layouts  0.63 us (2%)
    pallas_call x1, Pallas kernels, fused(): pl.pallas_call(functools.partial(layer_kernel, n_dp, n_e, cap, GROUPS, NE...  37.6 us

profile of v1, /device:TPU:0, one launch (start us, length us, event | category | flops | bytes accessed | tf_op | source)
XLA Modules:
  0.0 38.2 jit_solution(10412962758986218590)
XLA Ops:
  0.0 37.6 %shard_map.100 = bf16[16,1792]{1,0:T(8,128)(2,1)S(1)} custom-call(bf16[16,1792]{1,0:T(8,128)(2,1)} %x_hbm.1, bf16[16,1792]{1,0:T(8,128)(2,1)} %cur_hbm.1, s32[4,16]{1,0:T(4,128)} %bitcast.2, f32[4,16]{1,0:T(4,128)} %bitcast.3, bf16[1,1792,2048]{2,1,0:T(8,128)(2,1)} %gate_hbm.1, bf16[1,1792,2048]{2,1,0:T(8,128)(2,1)} %up_hbm.1, ...), custom_call_target="tpu_custom_call" | custom-call | tf_op jit(solution)/shard_map/pallas_call | solution.py:444
  37.6 0.6 %copy.12 = bf16[16,1792]{1,0:T(8,128)(2,1)} copy(bf16[16,1792]{1,0:T(8,128)(2,1)S(1)} %shard_map.100) | data formatting | bytes 114688

commit v2 on v1

--- a/solution.py
+++ b/solution.py
@@ -87,6 +87,7 @@
 BF = jnp.bfloat16
 F32 = jnp.float32
 PARTS = 2
+AROUND = (3, 1, 2, 0)
 
 
 def dot(a, b):
@@ -94,13 +95,13 @@
 
 
 def layer_kernel(
-    n_dp, n_e, cap, groups, near,
+    n_dp, n_e, cap, groups,
     x_hbm, cur_hbm, ids_hbm, w_hbm, gate_hbm, up_hbm, down_hbm, sg_hbm, su_hbm, sd_hbm,
     out_ref,
     gu_v, down_v, sgu_v, sd_v, ids_v, w_v, flip, xm, cm,
     xc, part, rs_in, hid, acc, shv, sh_part, sh_in, sh_hid, own_sum, contrib, pair_in, fin_out, fin_in,
     in_sem, gu_sem, down_sem, shw_sem,
-    snd, x_r, xp_r, c_r, cp_r, rs_s, rs_r, hid_s, hid_r, shp_r, shh_r, pair_r, fin_r,
+    snd, x_r, xp_r, cp_r, rs_s, rs_r, hid_s, hid_r, shp_r, shh_r, pair_r, fin_r,
 ):
     me_d = lax.axis_index("dp")
     me_e = lax.axis_index("expert")
@@ -113,9 +114,10 @@
     top = ids_hbm.shape[0]
     chunk = gu_v.shape[2] // 2
     hs = chunk * PARTS
-    shc = sgu_v.shape[1] // 2
+    shc = sgu_v.shape[2] // 2
     held = 2 * tokens
-    slots = [(q, s) for q in range(PARTS) for s in [*range(n_dp - 1, 0, -1), 0]]
+    slots = [(q, s) for q in range(PARTS) for s in AROUND]
+    place_of = {slot: i for i, slot in enumerate(slots)}
 
     def start(src, dst, sem):
         copy = pltpu.make_async_copy(src, dst, sem)
@@ -155,11 +157,13 @@
     got_w = start(w_hbm, w_v, in_sem.at[1])
     got_x = start(x_hbm, xm.at[c, :, pl.ds(0, width)], in_sem.at[2])
     got_cur = start(cur_hbm, cm.at[c], in_sem.at[3])
+    def shared_at(d):
+        return pl.ds(pl.multiple_of((c * n_dp + d) * shc, 128), shc)
+
     def fetch_shared():
-        mine = pl.ds(pl.multiple_of(lax.rem(me_e, 2 * near) * shc, 128), shc)
-        start(sg_hbm.at[:, mine], sgu_v.at[:, pl.ds(0, shc)], shw_sem.at[0])
-        start(su_hbm.at[:, mine], sgu_v.at[:, pl.ds(shc, shc)], shw_sem.at[0])
-        start(sd_hbm.at[mine, :], sd_v, shw_sem.at[1])
+        for i, s in enumerate(AROUND):
+            start(sg_hbm.at[:, shared_at(dp_dev(s))], sgu_v.at[i, :, pl.ds(0, shc)], shw_sem.at[i])
+            start(su_hbm.at[:, shared_at(dp_dev(s))], sgu_v.at[i, :, pl.ds(shc, shc)], shw_sem.at[i])
 
     def fetch_down():
         for q in range(PARTS):
@@ -167,6 +171,9 @@
                 row = pl.ds(pl.multiple_of(dp_src(s) * hs + q * chunk, 128), chunk)
                 start(down_hbm.at[0, row, :], down_v.at[pl.ds((q * n_dp + i) * chunk, chunk), :], down_sem.at[q])
 
+        for i, s in enumerate([*range(n_dp - 1, 0, -1), 0]):
+            start(sd_hbm.at[shared_at(dp_src(s)), :], sd_v.at[pl.ds(i * shc, shc), :], shw_sem.at[n_dp])
+
     def remote(src, dst, ssem, rsem, dp, e):
         pltpu.make_async_remote_copy(
             src_ref=src, dst_ref=dst, send_sem=ssem, recv_sem=rsem, device_id=(dp, e), device_id_type=MESH
@@ -175,6 +182,8 @@
     before = lax.broadcasted_iota(jnp.int32, (128, 128), 0) < lax.broadcasted_iota(jnp.int32, (128, 128), 1)
     before = jnp.where(before, 1.0, 0.0).astype(BF)
     flip[...] = jnp.zeros_like(flip)
+    for buf in xc:
+        buf[...] = jnp.zeros_like(buf)
     got_ids.wait()
     got_w.wait()
     flip[:top, :tokens] = ids_v[...].astype(F32)
@@ -199,21 +208,15 @@
         pl.semaphore_wait(barrier, n_dp - 1 + zs - 1 + 1)
 
     remote(xm.at[c], xm.at[c], snd.at[0], xp_r.at[0], me_d, partner)
-    for s in range(1, zs):
-        remote(xm.at[c], xm.at[2 * s + c], snd.at[0], x_r.at[s], me_d, z_dev(s))
+    for g in groups[1:]:
+        for s in g:
+            remote(xm.at[c], xm.at[2 * s + c], snd.at[0], x_r.at[s], me_d, z_dev(s))
     remote(cm.at[c], cm.at[c], snd.at[1], cp_r.at[0], me_d, partner)
-    for s in range(1, near):
-        remote(cm.at[c], cm.at[2 * s + c], snd.at[1], c_r.at[s], me_d, z_dev(s))
 
     def relay_x(s):
         with jax.named_scope(f"relay{s}"):
             landed(xm.at[2 * s + c], x_r.at[s])
         remote(xm.at[2 * s + c], xm.at[2 * s + c], snd.at[0], xp_r.at[s], me_d, partner)
-
-    def relay_cur(s):
-        with jax.named_scope(f"crelay{s}"):
-            landed(cm.at[2 * s + c], c_r.at[s])
-        remote(cm.at[2 * s + c], cm.at[2 * s + c], snd.at[1], cp_r.at[s], me_d, partner)
 
     me_f = me_e.astype(F32)
 
@@ -240,27 +243,39 @@
         place = jnp.where(jnp.logical_and(place == rank, scale > 0), 1.0, 0.0)
         size = held * len(groups[g])
         source = jnp.concatenate([xm[2 * s:2 * s + 2, :, :width].reshape(held, width) for s in groups[g]], axis=0)
-        xc[g][...] = dot(place[:, :size].astype(BF), source).astype(BF)
+        xc[g][:padded] = dot(place[:, :size].astype(BF), source).astype(BF)
         return place, scale
 
     def gate_up(g, hooks):
         rows = part[g].shape[1]
-        for i, (q, s) in enumerate(slots):
+        value = None
+
+        def ship(i, value):
+            q, s = slots[i]
+            part[g][i] = value[:rows].astype(BF)
+            if s:
+                remote(part[g].at[i], rs_in[g].at[q * (n_dp - 1) + s - 1], rs_s.at[g], rs_r.at[PARTS * g + q], dp_dev(s), me_e)
+
+        for i in range(len(slots)):
             if g == 0:
-                with jax.named_scope(f"w{i}"):
-                    landed(gu_v.at[i], gu_sem.at[i])
-            part[g][i] = dot(xc[g][...], gu_v[i])[:rows].astype(BF)
-            if s:
-                remote(part[g].at[i], rs_in[g].at[i], rs_s.at[g], rs_r.at[PARTS * g + q], dp_dev(s), me_e)
+                landed(gu_v.at[i], gu_sem.at[i])
+            following = dot(xc[g][...], gu_v[i])
+            if not DEFER:
+                ship(i, following)
+            elif i:
+                ship(i - 1, value)
+            value = following
             for hook in hooks.get(i, ()):
                 hook()
+        if DEFER:
+            ship(len(slots) - 1, value)
 
     def back(g, place, scale):
         rows = part[g].shape[1]
         size = held * len(groups[g])
         tall = jnp.concatenate([place, jnp.zeros((128 - place.shape[0], 128), F32)], axis=0)
         turned = jnp.transpose(tall)[:size]
-        weight = jnp.sum(place * scale, axis=1, keepdims=True)[:rows]
+        weight = jnp.sum(place[:rows] * scale, axis=1, keepdims=True)
         return turned[:, :rows].astype(BF), weight
 
     def gated(term, n):
@@ -269,86 +284,95 @@
 
     def act(g, q):
         base = q * n_dp
-        others = pl.ds(base, n_dp - 1)
         with jax.named_scope(f"rs{g}{q}"):
-            landed(rs_in[g].at[others], rs_r.at[PARTS * g + q])
-        term = part[g][base + n_dp - 1].astype(F32)
+            landed(rs_in[g].at[pl.ds(q * (n_dp - 1), n_dp - 1)], rs_r.at[PARTS * g + q])
+        term = part[g][place_of[q, 0]].astype(F32)
         for s in range(1, n_dp):
-            term = term + rs_in[g][base + n_dp - 1 - s].astype(F32)
+            term = term + rs_in[g][q * (n_dp - 1) + s - 1].astype(F32)
         own = base + n_dp - 1
         hid[g][own] = gated(term, chunk)
         for s in range(1, n_dp):
             remote(hid[g].at[own], hid[g].at[base + n_dp - 1 - s], hid_s.at[g], hid_r.at[PARTS * g + q], dp_dev(s), me_e)
 
-    def down(g, weight, between=None):
-        span = n_dp * chunk
-
-        def gathered(q):
-            with jax.named_scope(f"hid{g}{q}"):
-                landed(hid[g].at[pl.ds(q * n_dp, n_dp - 1)], hid_r.at[PARTS * g + q])
-            if g == 0:
-                landed(down_v.at[pl.ds(q * span, span), :], down_sem.at[q])
-            return [hid[g][q * n_dp + i] for i in range(n_dp)]
-
-        rows = part[g].shape[1]
-        if between is not None:
-            for q in range(PARTS):
-                value = dot(jnp.concatenate(gathered(q), axis=1), down_v[q * span:(q + 1) * span])
-                if q < PARTS - 1:
-                    acc[:rows] = value if q == 0 else acc[:rows] + value
-                    between()
-            value = acc[:rows] + value
-        else:
-            pieces = [piece for q in range(PARTS) for piece in gathered(q)]
-            value = dot(jnp.concatenate(pieces, axis=1), down_v[...])
-        return (weight * value).astype(BF)
-
-    def give(g, turned, value):
+    span = n_dp * chunk
+    half = width // HALVES
+
+    def gathered(g, q):
+        with jax.named_scope(f"hid{g}{q}"):
+            landed(hid[g].at[pl.ds(q * n_dp, n_dp - 1)], hid_r.at[PARTS * g + q])
+        if g == 1:
+            landed(down_v.at[pl.ds(q * span, span), :], down_sem.at[q])
+        return [hid[g][q * n_dp + i] for i in range(n_dp)]
+
+    def down(g, weight):
+        pieces = [piece for q in range(PARTS) for piece in gathered(g, q)]
+        return (weight * dot(jnp.concatenate(pieces, axis=1), down_v[...])).astype(BF)
+
+    def down_first(g):
+        acc[...] = dot(jnp.concatenate(gathered(g, 0), axis=1), down_v[:span])
+
+    def down_rest(g):
+        return jnp.concatenate(gathered(g, 1), axis=1)
+
+    def give(g, turned, value, h=None):
+        cols = slice(0, width) if h is None else slice(h * half, (h + 1) * half)
         value = dot(turned, value)
         for k, s in enumerate(groups[g]):
-            one = value[k * held:(k + 1) * held].reshape(2, tokens, width)
-            if s < near:
-                one = one + shv[2 * s:2 * s + 2]
-            contrib[s] = one.astype(BF)
-            remote(contrib.at[s, 1 - c], pair_in.at[s], snd.at[4], pair_r.at[s], me_d, partner)
-
-    def settle(s):
-        with jax.named_scope(f"pair{s}"):
-            landed(pair_in.at[s], pair_r.at[s])
-        summed = contrib[s, c].astype(F32) + pair_in[s].astype(F32)
+            one = value[k * held:(k + 1) * held]
+            if s == 0:
+                one = one + shv[...]
+            one = one.astype(BF).reshape(2, tokens, -1)
+            for j in range(HALVES) if h is None else (h,):
+                contrib[s, j] = one[:, :, j * half:(j + 1) * half] if h is None else one
+                remote(contrib.at[s, j, 1 - c], pair_in.at[s, j], snd.at[4], pair_r.at[HALVES * s + j], me_d, partner)
+
+    def settle(s, j):
+        with jax.named_scope(f"pair{s}{j}"):
+            landed(pair_in.at[s, j], pair_r.at[HALVES * s + j])
+        summed = contrib[s, j, c].astype(F32) + pair_in[s, j].astype(F32)
         if s:
-            fin_out[s - 1] = summed.astype(BF)
-            remote(fin_out.at[s - 1], fin_in.at[s - 1], snd.at[5], fin_r.at[s], me_d, z_src(s))
+            fin_out[s - 1, j] = summed.astype(BF)
+            remote(fin_out.at[s - 1, j], fin_in.at[s - 1, j], snd.at[5], fin_r.at[HALVES * s + j], me_d, z_src(s))
         else:
-            own_sum[...] = summed
-
-    def shared_up():
-        for s in range(near):
-            with jax.named_scope(f"ccoll{s}"):
-                landed(cm.at[2 * s + 1 - c], cp_r.at[s])
-        with jax.named_scope("shw"):
-            landed(sgu_v, shw_sem.at[0])
-        cur = cm[...].reshape(near * held, width)
-        sh_part[...] = dot(cur, sgu_v[...]).astype(BF).reshape(sh_part.shape)
-        for s in range(1, n_dp):
-            remote(sh_part.at[dp_dev(s)], sh_in.at[s - 1], snd.at[2], shp_r.at[0], dp_dev(s), me_e)
+            own_sum[:, j * half:(j + 1) * half] = summed
+
+    def shared_up(lo, hi):
+        if lo == 0:
+            with jax.named_scope("ccoll"):
+                landed(cm.at[1 - c], cp_r.at[0])
+        cur = cm[...].reshape(held, width)
+        value = None
+
+        def ship(i, value):
+            s = AROUND[i]
+            sh_part[i] = value.astype(BF)
+            if s:
+                remote(sh_part.at[i], sh_in.at[s - 1], snd.at[2], shp_r.at[0], dp_dev(s), me_e)
+
+        for i in range(lo, hi):
+            with jax.named_scope(f"shw{i}"):
+                landed(sgu_v.at[i], shw_sem.at[i])
+            following = dot(cur, sgu_v[i])
+            if i > lo:
+                ship(i - 1, value)
+            value = following
+        ship(hi - 1, value)
 
     def shared_act():
         with jax.named_scope("shrs"):
             landed(sh_in, shp_r.at[0])
-        term = sh_part[me_d].astype(F32)
+        term = sh_part[n_dp - 1].astype(F32)
         for s in range(1, n_dp):
             term = term + sh_in[s - 1].astype(F32)
-        sh_hid[me_d] = gated(term, shc)
+        sh_hid[n_dp - 1] = gated(term, shc)
         for s in range(1, n_dp):
-            remote(sh_hid.at[me_d], sh_hid.at[me_d], snd.at[3], shh_r.at[s], dp_dev(s), me_e)
+            remote(sh_hid.at[n_dp - 1], sh_hid.at[n_dp - 1 - s], snd.at[3], shh_r.at[0], dp_dev(s), me_e)
 
     def shared_down():
-        for s in range(1, n_dp):
-            with jax.named_scope(f"shh{s}"):
-                landed(sh_hid.at[dp_src(s)], shh_r.at[s])
-        landed(sd_v, shw_sem.at[1])
-        shv[...] = dot(sh_hid[...].reshape(near * held, shc), sd_v[...]).reshape(shv.shape)
+        with jax.named_scope("shh"):
+            landed(sh_hid.at[pl.ds(0, n_dp - 1)], shh_r.at[0])
+        landed(sd_v, shw_sem.at[n_dp])
+        shv[...] = dot(jnp.concatenate([sh_hid[i] for i in range(n_dp)], axis=1), sd_v[...])
 
     order = list(range(len(groups)))
     kept = {}
@@ -357,40 +381,54 @@
         return [functools.partial(*call) for call in calls]
 
     hooks = [
-        {2: do((fetch_shared,)), 4: do((fetch_down,)), 6: do((relay_x, 1))},
-        {2: do((act, 0, 0)), 4: do((act, 0, 1), (relay_x, 2)), 5: do((relay_cur, 1)), 6: do((relay_x, 3))},
-        {},
+        {0: do((fetch_shared,)), 3: do((fetch_down,)), 6: do((relay_x, 1))},
+        {2: do((relay_x, 3))},
+        {1: do((relay_x, 2))},
+        {2: do((act, 1, 1))},
     ]
     for g in order:
         place, scale = route(g)
         gate_up(g, hooks[g])
         kept[g] = back(g, place, scale)
-        if g == 1:
-            shared_up()
-    for q in range(PARTS):
-        act(1, q)
-    shared_act()
-    first_value = down(0, kept[0][1])
+        if g == 0:
+            shared_up(0, 2)
+        if g == 2:
+            act(1, 0)
     act(2, 0)
     act(2, 1)
-    second_value = down(1, kept[1][1])
+    shared_up(2, n_dp)
+    act(3, 0)
+    act(3, 1)
+    act(0, 0)
+    act(0, 1)
+    give(1, kept[1][0], down(1, kept[1][1]))
+    give(2, kept[2][0], down(2, kept[2][1]))
+    shared_act()
+    down_first(3)
+    for j in range(HALVES):
+        settle(1, j)
+    for j in range(HALVES):
+        settle(3, j)
+    lhs = down_rest(3)
+    turned, weight = kept[3]
+    for j in range(HALVES):
+        cols = slice(j * half, (j + 1) * half)
+        value = acc[:, cols] + dot(lhs, down_v[span:, cols])
+        give(3, turned, (weight * value).astype(BF), j)
+    for j in range(HALVES):
+        settle(2, j)
     shared_down()
-    give(0, kept[0][0], first_value)
-    give(1, kept[1][0], second_value)
-
-    def near_home():
-        settle(1)
-        settle(0)
-
-    give(2, kept[2][0], down(2, kept[2][1], near_home))
-    settle(3)
-    settle(2)
-    both = own_sum[...]
-    for s in range(1, zs):
-        with jax.named_scope(f"fin{s}"):
-            landed(fin_in.at[s - 1], fin_r.at[s])
-        both = both + fin_in[s - 1].astype(F32)
-    out_ref[...] = both.astype(BF)
+    give(0, kept[0][0], down(0, kept[0][1]))
+    for j in range(HALVES):
+        settle(0, j)
+    for j in range(HALVES):
+        cols = slice(j * half, (j + 1) * half)
+        both = own_sum[:, cols]
+        for s in range(1, zs):
+            with jax.named_scope(f"fin{s}{j}"):
+                landed(fin_in.at[s - 1, j], fin_r.at[HALVES * s + j])
+            both = both + fin_in[s - 1, j].astype(F32)
+        out_ref[:, cols] = both.astype(BF)
 
     def sent(ref, sem):
         pltpu.make_async_remote_copy(
@@ -399,7 +437,7 @@
 
     with jax.named_scope("sendwait"):
         sent(xm.at[pl.ds(0, 2 * zs - 1)], snd.at[0])
-        sent(cm.at[pl.ds(0, 2 * near - 1)], snd.at[1])
+        sent(cm.at[0], snd.at[1])
         sent(sh_part.at[pl.ds(0, n_dp - 1)], snd.at[2])
         sent(sh_hid.at[pl.ds(0, n_dp - 1)], snd.at[3])
         sent(pair_in, snd.at[4])
@@ -409,8 +447,9 @@
             sent(hid[g].at[pl.ds(0, PARTS * (n_dp - 1))], hid_s.at[g])
 
 
-GROUPS = ((0,), (1,), (2, 3))
-NEAR = 2
+GROUPS = ((0,), (1,), (3,), (2,))
+HALVES = 1
+DEFER = True
 
 
 def fused(n_dp, n_e, shortcut_in, current_in, expert_ids, route_weight, gate_weight, up_weight, down_weight, shared_gate, shared_up, shared_down):
@@ -421,28 +460,30 @@
     chunk = hidden // n_dp // PARTS
     count = PARTS * n_dp
     zs = n_e // 2
-    shc = hidden // (2 * NEAR)
-    share = 2 * NEAR * tokens // n_dp
+    shc = hidden // (2 * n_dp)
+    held = 2 * tokens
     rows = [2 * cap * len(g) for g in GROUPS]
     n_g = len(GROUPS)
     V = pltpu.VMEM
     S = pltpu.SemaphoreType.DMA
     scratch = [
-        V((count, width, 2 * chunk), BF), V((hidden, width), BF), V((width, 2 * shc), BF), V((shc, width), BF),
+        V((count, width, 2 * chunk), BF), V((hidden, width), BF), V((n_dp, width, 2 * shc), BF), V((n_dp * shc, width), BF),
         V((top, tokens), jnp.int32), V((top, tokens), F32), V((tokens, 128), F32),
-        V((n_e, tokens, width + 128), BF), V((2 * NEAR, tokens, width), BF),
-        [V((-(-r // 16) * 16, width), BF) for r in rows], [V((count, r, 2 * chunk), BF) for r in rows], [V((count, r, 2 * chunk), BF) for r in rows], [V((count, r, chunk), BF) for r in rows],
-        V((max(rows), width), F32), V((2 * NEAR, tokens, width), F32),
-        V((n_dp, share, 2 * shc), BF), V((n_dp - 1, share, 2 * shc), BF), V((n_dp, share, shc), BF), V((tokens, width), F32),
-        V((zs, 2, tokens, width), BF), V((zs, tokens, width), BF), V((zs - 1, tokens, width), BF), V((zs - 1, tokens, width), BF),
-        S((4,)), S((count,)), S((PARTS,)), S((2,)),
-        S((6,)), S((zs,)), S((zs,)), S((NEAR,)), S((NEAR,)),
-        S((n_g,)), S((PARTS * n_g,)), S((n_g,)), S((PARTS * n_g,)), S((1,)), S((n_dp,)), S((zs,)), S((zs,)),
+        V((n_e, tokens, width + 128), BF), V((2, tokens, width), BF),
+        [V((128, width), BF) for r in rows], [V((count, r, 2 * chunk), BF) for r in rows],
+        [V((PARTS * (n_dp - 1), r, 2 * chunk), BF) for r in rows], [V((count, r, chunk), BF) for r in rows],
+        V((rows[-1], width), F32), V((held, width), F32),
+        V((n_dp, held, 2 * shc), BF), V((n_dp - 1, held, 2 * shc), BF), V((n_dp, held, shc), BF), V((tokens, width), F32),
+        V((zs, HALVES, 2, tokens, width // HALVES), BF), V((zs, HALVES, tokens, width // HALVES), BF),
+        *[V((zs - 1, HALVES, tokens, width // HALVES), BF) for _ in range(2)],
+        S((4,)), S((count,)), S((PARTS,)), S((n_dp + 1,)),
+        S((6,)), S((zs,)), S((zs,)), S((1,)),
+        S((n_g,)), S((PARTS * n_g,)), S((n_g,)), S((PARTS * n_g,)), S((1,)), S((1,)), S((HALVES * zs,)), S((HALVES * zs,)),
     ]
     vm = pl.BlockSpec(memory_space=pltpu.VMEM)
     hbm = pl.BlockSpec(memory_space=pl.ANY)
     return pl.pallas_call(
-        functools.partial(layer_kernel, n_dp, n_e, cap, GROUPS, NEAR),
+        functools.partial(layer_kernel, n_dp, n_e, cap, GROUPS),
         out_shape=pltpu.VMEM((tokens, width), BF),
         in_specs=[hbm] * 10,
         out_specs=vm,
@@ -456,9 +497,9 @@
     top = arrays[2].shape[1]
     experts, _, hidden = arrays[4].shape
     aligned = (
-        experts == 1 and n_e == 2 * sum(len(g) for g in GROUPS) and 4 * top <= tokens and tokens == 16 and width % 128 == 0
-        and hidden % (n_dp * PARTS * 128) == 0 and hidden % (2 * NEAR * 128) == 0
-        and 2 * NEAR * tokens % (n_dp * 16) == 0 and 3 * tokens * top % (2 * n_e) == 0 and 2 * (3 * tokens * top // (2 * n_e)) % 8 == 0
+        experts == 1 and n_dp == 4 and n_e == 2 * sum(len(g) for g in GROUPS) and 4 * top <= tokens and tokens == 16 and width % (HALVES * 128) == 0
+        and hidden % (n_dp * PARTS * 128) == 0 and hidden % (2 * n_dp * 128) == 0
+        and 3 * tokens * top % (2 * n_e) == 0 and 2 * (3 * tokens * top // (2 * n_e)) % 8 == 0
     )
     return fused(n_dp, n_e, *arrays) if aligned else local(*arrays)
 

time: 38.4 us -> 35.9 us (0.935)
  Pallas kernels: 37.6 us -> 35.1 us
    pallas_call x1, Pallas kernels: 37.6 us -> 35.1 us  [fused(): pl.pallas_call(functools.partial(layer_kernel, n_dp, n_e, cap, GROUPS), o...]
where the time goes in v2:
time: 35.9 us; the launch traced here: 35.7 us
  Pallas kernels  35.1 us (98%)
  local copies, waits for them, and re-layouts  0.63 us (2%)
    pallas_call x1, Pallas kernels, fused(): pl.pallas_call(functools.partial(layer_kernel, n_dp, n_e, cap, GROUPS), o...  35.1 us

profile of v2, /device:TPU:0, one launch (start us, length us, event | category | flops | bytes accessed | tf_op | source)
XLA Modules:
  0.0 35.7 jit_solution(7290745072374919220)
XLA Ops:
  0.0 35.1 %shard_map.100 = bf16[16,1792]{1,0:T(8,128)(2,1)S(1)} custom-call(bf16[16,1792]{1,0:T(8,128)(2,1)} %x_hbm.1, bf16[16,1792]{1,0:T(8,128)(2,1)} %cur_hbm.1, s32[4,16]{1,0:T(4,128)} %bitcast.2, f32[4,16]{1,0:T(4,128)} %bitcast.3, bf16[1,1792,2048]{2,1,0:T(8,128)(2,1)} %gate_hbm.1, bf16[1,1792,2048]{2,1,0:T(8,128)(2,1)} %up_hbm.1, ...), custom_call_target="tpu_custom_call" | custom-call | tf_op jit(solution)/shard_map/pallas_call | solution.py:485
  35.1 0.6 %copy.12 = bf16[16,1792]{1,0:T(8,128)(2,1)} copy(bf16[16,1792]{1,0:T(8,128)(2,1)S(1)} %shard_map.100) | data formatting | bytes 114688

commit v3 on v2

--- a/solution.py
+++ b/solution.py
@@ -116,6 +116,7 @@
     hs = chunk * PARTS
     shc = sgu_v.shape[2] // 2
     held = 2 * tokens
+    named_rows = -(-n_e // 16) * 16
     slots = [(q, s) for q in range(PARTS) for s in AROUND]
     place_of = {slot: i for i, slot in enumerate(slots)}
 
@@ -186,7 +187,18 @@
         buf[...] = jnp.zeros_like(buf)
     got_ids.wait()
     got_w.wait()
-    flip[:top, :tokens] = ids_v[...].astype(F32)
+    ids = ids_v[...].astype(F32)
+    flip[:top, :tokens] = ids
+    numbers = lax.broadcasted_iota(jnp.int32, (named_rows, 128), 0).astype(F32)
+    spread_ids = flip[:top, :]
+    inside = lax.broadcasted_iota(jnp.int32, (named_rows, 128), 1) < tokens
+    taken = jnp.zeros((named_rows, 128), F32)
+    for k in range(top):
+        taken = taken + jnp.where(jnp.logical_and(spread_ids[k:k + 1] == numbers, inside), 1.0, 0.0)
+    ranks = dot(taken.astype(BF), before)
+    for k in range(top):
+        rank = jnp.sum(jnp.where(spread_ids[k:k + 1] == numbers, ranks, 0.0), axis=0, keepdims=True)
+        flip[k:k + 1, :] = spread_ids[k:k + 1] * STRIDE + rank
     flip[top:2 * top, :tokens] = w_v[...]
     named = flip[...]
     named = jnp.where(c == 1, pltpu.roll(named, tokens, 1), named)
@@ -223,7 +235,10 @@
     def chosen(block):
         table = xm[block, :, width:].astype(F32)
         weight = table[top:2 * top] + table[2 * top:3 * top] + table[3 * top:4 * top]
-        return jnp.sum(jnp.where(table[:top] == me_f, weight, 0.0), axis=0, keepdims=True)
+        offset = table[:top] - me_f * STRIDE
+        mine = jnp.logical_and(jnp.logical_and(offset >= 0, offset < STRIDE), weight > 0)
+        scale = jnp.sum(jnp.where(mine, weight, 0.0), axis=0, keepdims=True)
+        return scale, jnp.sum(jnp.where(mine, offset + (block % 2) * cap, 0.0), axis=0, keepdims=True)
 
     def route(g):
         rows = part[g].shape[1]
@@ -231,14 +246,13 @@
         for s in groups[g]:
             with jax.named_scope(f"coll{s}"):
                 landed(xm.at[2 * s + 1 - c], xp_r.at[s])
-        scale = None
+        scale = rank = None
         for k, s in enumerate(groups[g]):
-            one = chosen(2 * s) + chosen(2 * s + 1)
-            one = pltpu.roll(one, held * k, 1) if k else one
-            scale = one if scale is None else scale + one
-        scale = jnp.broadcast_to(scale, (8, 128))
-        rank = dot(jnp.where(scale > 0, 1.0, 0.0).astype(BF), before)[:1]
-        scale = scale[:1]
+            pair = [chosen(2 * s), chosen(2 * s + 1)]
+            one = [pair[0][n] + pair[1][n] for n in (0, 1)]
+            one[1] = one[1] + jnp.where(one[0] > 0, 2 * cap * k, 0.0) if k else one[1]
+            one = [pltpu.roll(row, held * k, 1) for row in one] if k else one
+            scale, rank = one if scale is None else (scale + one[0], rank + one[1])
         place = lax.broadcasted_iota(jnp.int32, (padded, 128), 0).astype(F32)
         place = jnp.where(jnp.logical_and(place == rank, scale > 0), 1.0, 0.0)
         size = held * len(groups[g])
@@ -384,31 +398,30 @@
         {0: do((fetch_shared,)), 3: do((fetch_down,)), 6: do((relay_x, 1))},
         {2: do((relay_x, 3))},
         {1: do((relay_x, 2))},
-        {2: do((act, 1, 1))},
+        {1: do((act, 1, 0)), 3: do((act, 1, 1))},
     ]
     for g in order:
         place, scale = route(g)
         gate_up(g, hooks[g])
         kept[g] = back(g, place, scale)
         if g == 0:
-            shared_up(0, 2)
-        if g == 2:
-            act(1, 0)
+            shared_up(0, 1)
     act(2, 0)
     act(2, 1)
-    shared_up(2, n_dp)
+    shared_up(1, n_dp)
     act(3, 0)
     act(3, 1)
     act(0, 0)
     act(0, 1)
-    give(1, kept[1][0], down(1, kept[1][1]))
+    second_value = down(1, kept[1][1])
     give(2, kept[2][0], down(2, kept[2][1]))
+    give(1, kept[1][0], second_value)
     shared_act()
     down_first(3)
     for j in range(HALVES):
+        settle(3, j)
+    for j in range(HALVES):
         settle(1, j)
-    for j in range(HALVES):
-        settle(3, j)
     lhs = down_rest(3)
     turned, weight = kept[3]
     for j in range(HALVES):
@@ -449,6 +462,7 @@
 
 GROUPS = ((0,), (1,), (3,), (2,))
 HALVES = 1
+STRIDE = 16
 DEFER = True
 
 
@@ -497,7 +511,7 @@
     top = arrays[2].shape[1]
     experts, _, hidden = arrays[4].shape
     aligned = (
-        experts == 1 and n_dp == 4 and n_e == 2 * sum(len(g) for g in GROUPS) and 4 * top <= tokens and tokens == 16 and width % (HALVES * 128) == 0
+        experts == 1 and n_dp == 4 and n_e == 2 * sum(len(g) for g in GROUPS) and 4 * top <= tokens and tokens == STRIDE and n_e * STRIDE <= 256 and width % (HALVES * 128) == 0
         and hidden % (n_dp * PARTS * 128) == 0 and hidden % (2 * n_dp * 128) == 0
         and 3 * tokens * top % (2 * n_e) == 0 and 2 * (3 * tokens * top // (2 * n_e)) % 8 == 0
     )

time: 35.9 us -> 35.1 us (0.978)
  Pallas kernels: 35.1 us -> 34.3 us
    pallas_call x1, Pallas kernels: 35.1 us -> 34.3 us  [fused(): pl.pallas_call(functools.partial(layer_kernel, n_dp, n_e, cap, GROUPS), o...]
where the time goes in v3:
time: 35.1 us; the launch traced here: 35 us
  Pallas kernels  34.3 us (98%)
  local copies, waits for them, and re-layouts  0.63 us (2%)
    pallas_call x1, Pallas kernels, fused(): pl.pallas_call(functools.partial(layer_kernel, n_dp, n_e, cap, GROUPS), o...  34.3 us

profile of v3, /device:TPU:0, one launch (start us, length us, event | category | flops | bytes accessed | tf_op | source)
XLA Modules:
  0.0 35.0 jit_solution(2520714466793783525)
XLA Ops:
  0.0 34.3 %shard_map.100 = bf16[16,1792]{1,0:T(8,128)(2,1)S(1)} custom-call(bf16[16,1792]{1,0:T(8,128)(2,1)} %x_hbm.1, bf16[16,1792]{1,0:T(8,128)(2,1)} %cur_hbm.1, s32[4,16]{1,0:T(4,128)} %bitcast.2, f32[4,16]{1,0:T(4,128)} %bitcast.3, bf16[1,1792,2048]{2,1,0:T(8,128)(2,1)} %gate_hbm.1, bf16[1,1792,2048]{2,1,0:T(8,128)(2,1)} %up_hbm.1, ...), custom_call_target="tpu_custom_call" | custom-call | tf_op jit(solution)/shard_map/pallas_call | solution.py:499
  34.4 0.6 %copy.12 = bf16[16,1792]{1,0:T(8,128)(2,1)} copy(bf16[16,1792]{1,0:T(8,128)(2,1)S(1)} %shard_map.100) | data formatting | bytes 114688
